TPU v7x, 32 devices: a whole 2x2x4 slice. The times are simulated.
32 devices in a mesh: ga: 2 (over x), ta: 4 (over y, core), gy: 4 (over z).
Axes of the slice: x: 2, y: 2, z: 4, core: 2. Of those that a mesh axis runs over, the one named last changes fastest.
Arguments:
- clip: bfloat16 [32, 16, 64, 512], P(('ga', 'ta'), 'gy'), parts along dimension 0, may hold values from -6 to 6
- w_space: bfloat16 [3, 3, 512, 512], replicated, may hold values from -0.09375 to 0.09375
- w_time: bfloat16 [3, 512, 512], replicated, may hold values from -0.15625 to 0.15625
- w_qkv: bfloat16 [512, 1536], replicated, may hold values from -0.61871843 to 0.61871843
- w_out: bfloat16 [512, 512], replicated, may hold values from -0.25 to 0.25
- norm_gain: float32 [512], replicated, may hold values from 0.1 to 1.9
Outputs:
- block_out: bfloat16 [32, 16, 64, 512], P(('ga', 'ta'), 'gy'), parts along dimension 0
There are 2 independent parts, one for each index of `ga`. A program takes and returns all parts, laid end to end along the dimension named above; an argument that names none is the same for every part. Nothing has to cross between parts.
All inputs are finite; a program needn't handle non-finite values.
Results may differ from a plain program's by a relative error of at most 0.0085.
Values may be sent and summed in bfloat16 or wider, within the bound.
No kernel may reach another device: no remote copies, remote signals or barrier semaphores. Data moves between devices by JAX's collectives and lax.ppermute only.
A program may use at most 64 MiB of HBM per device.

v0:
```python
import jax
import jax.numpy as jnp
from jax import lax
from jax.sharding import PartitionSpec as P

HEADS = 8


def padded_2(block, sides, width):
    for axis, dim in sides:
        count = lax.axis_size(axis)
        forward = [(i, i + 1) for i in range(count - 1)]
        backward = [(target, source) for source, target in forward]
        low = lax.ppermute(
            lax.slice_in_dim(block, block.shape[dim] - width, None, axis=dim), axis, forward
        )
        high = lax.ppermute(lax.slice_in_dim(block, 0, width, axis=dim), axis, backward)
        block = jnp.concatenate([low, block, high], axis=dim)
    return block


def from_behind(array, axis, by):
    devices = lax.axis_size(axis)
    pairs = [(i, i + by) for i in range(devices) if 0 <= i + by < devices]
    return lax.ppermute(array, axis, pairs)


def conv_space(padded, w_space, height, width):
    channels = padded.shape[-1]
    total = jnp.zeros(padded.shape[:1] + (height, width, channels), jnp.float32)
    for row_off in range(3):
        for col_off in range(3):
            window = padded[:, row_off : row_off + height, col_off : col_off + width, :]
            product = jnp.dot(
                window.reshape(-1, channels),
                w_space[row_off, col_off],
                preferred_element_type=jnp.float32,
            )
            total = total + product.reshape(total.shape)
    return total


def temporal_mix(clip, hidden, earlier, w_time, norm_gain):
    channels = clip.shape[-1]
    frames = hidden.shape[0]
    joined = jnp.concatenate([earlier, hidden], axis=0)
    total = jnp.zeros(hidden.shape, jnp.float32)
    for tap_index in range(3):
        window = joined[2 - tap_index : 2 - tap_index + frames]
        product = jnp.dot(
            window.reshape(-1, channels), w_time[tap_index], preferred_element_type=jnp.float32
        )
        total = total + product.reshape(hidden.shape)
    mixed = (clip.astype(jnp.float32) + total).astype(jnp.bfloat16)
    wide = mixed.astype(jnp.float32)
    scale = lax.rsqrt(jnp.mean(wide * wide, axis=-1, keepdims=True) + 1e-06)
    normed = (wide * scale * norm_gain).astype(jnp.bfloat16)
    return (mixed, normed)


def project(normed, w_qkv):
    channels = normed.shape[-1]
    flattened = jnp.dot(
        normed.reshape(-1, channels), w_qkv, preferred_element_type=jnp.float32
    ).astype(jnp.bfloat16)
    joined = flattened.reshape(normed.shape[:-1] + (3 * channels,))
    return (
        joined[..., :channels],
        joined[..., channels : 2 * channels],
        joined[..., 2 * channels :],
    )


def attend(queries, keyset, valueset, heads):
    frames, rows, cols, channels = queries.shape
    head_dim = channels // heads
    shape = (frames, rows, cols, heads, head_dim)
    scores = jnp.einsum(
        "frwhd,grwhd->rwhfg",
        queries.reshape(shape),
        keyset.reshape(shape),
        preferred_element_type=jnp.float32,
    )
    scores = scores * (1.0 / head_dim**0.5)
    peak = jnp.max(scores, axis=-1, keepdims=True)
    expo = jnp.exp(scores - peak)
    probs = (expo / jnp.sum(expo, axis=-1, keepdims=True)).astype(jnp.bfloat16)
    output = jnp.einsum(
        "rwhfg,grwhd->frwhd", probs, valueset.reshape(shape), preferred_element_type=jnp.float32
    )
    return output.reshape(queries.shape).astype(jnp.bfloat16)


def attend_back(queries, keyset, valueset):
    output = attend(queries, keyset, valueset, HEADS)
    return lax.all_to_all(output, "ta", split_axis=0, concat_axis=2, tiled=True)


def per_device(clip, w_space, w_time, w_qkv, w_out, norm_gain):
    frames, height, width, channels = clip.shape
    rimmed = padded_2(clip, (("gy", 1),), 1)
    padded = jnp.pad(rimmed, ((0, 0), (0, 0), (1, 1), (0, 0)))
    hidden = jax.nn.silu(conv_space(padded, w_space, height, width)).astype(jnp.bfloat16)
    earlier = from_behind(hidden[-2:], "ta", 1)
    mixed, normed = temporal_mix(clip, hidden, earlier, w_time, norm_gain)
    queries, keyset, valueset = project(
        lax.all_to_all(normed, "ta", split_axis=2, concat_axis=0, tiled=True), w_qkv
    )
    attended = attend_back(queries, keyset, valueset)
    projected = jnp.dot(
        attended.reshape(-1, channels), w_out, preferred_element_type=jnp.float32
    ).reshape(clip.shape)
    return (mixed.astype(jnp.float32) + projected).astype(jnp.bfloat16)


def solution(mesh):
    in_specs = (P(("ga", "ta"), "gy", None, None), P(), P(), P(), P(), P())
    out_specs = P(("ga", "ta"), "gy", None, None)
    return jax.shard_map(
        per_device, mesh=mesh, in_specs=in_specs, out_specs=out_specs, check_vma=False
    )
```

profile of v0, /device:TPU:0, one launch (start us, length us, event | category | flops | bytes accessed | tf_op | source)
XLA Modules:
  0.0 112.8 jit_solution(17687621035857392692)
XLA Ops:
  0.0 0.0 copy-start
  0.0 1.2 %fusion.79 = (bf16[4,1,64,512]{3,2,1,0:T(8,128)(2,1)S(1)}, bf16[4,1,64,512]{3,2,1,0:T(8,128)(2,1)S(1)}) fusion(bf16[4,4,64,512]{3,2,1,0:T(8,128)(2,1)} %param.6), kind=kLoop, calls=%fused_computation.87 | loop fusion | bytes 1048576 | tf_op jit(solution)/shard_map/slice | solution.py:15
  1.2 5.0 %collective-permute-start = (bf16[4,1,64,512]{3,2,1,0:T(8,128)(2,1)S(1)}, bf16[4,1,64,512]{3,2,1,0:T(8,128)(2,1)S(1)}, u32[]{:S(2)}, u32[]{:S(2)}) collective-permute-start(bf16[4,1,64,512]{3,2,1,0:T(8,128)(2,1)S(1)} %get-tuple-element.8), channel_id=1, source_target_pairs={{0,1},{1,2},{2,3},{4,5},{5,6},{6,7},{8,9},{9,10},{10,11},{12,13},{... | collective-permute-start | bytes 786440 | tf_op jit(solution)/shard_map/ppermute | solution.py:14
  6.2 0.0 copy-start.2
  6.2 1.4 %collective-permute-start.1 = (bf16[4,1,64,512]{3,2,1,0:T(8,128)(2,1)S(1)}, bf16[4,1,64,512]{3,2,1,0:T(8,128)(2,1)S(1)}, u32[]{:S(2)}, u32[]{:S(2)}) collective-permute-start(bf16[4,1,64,512]{3,2,1,0:T(8,128)(2,1)S(1)} %get-tuple-element.9), channel_id=1, source_target_pairs={{1,0},{2,1},{3,2},{5,4},{6,5},{7,6},{9,8},{10,9},{11,10},{13,12},{... | collective-permute-start | bytes 786440 | tf_op jit(solution)/shard_map/ppermute | solution.py:17
  7.6 0.0 copy-start.4
  7.6 2.2 %fusion.55 = f32[4,4,64,512]{3,2,1,0:T(8,128)S(1)} fusion(bf16[4,4,64,512]{3,2,1,0:T(8,128)(2,1)} %param.6, bf16[3,3,512,512]{3,2,1,0:T(8,128)(2,1)} %param.7), kind=kOutput, calls=%fused_computation.62 | convolution fusion | flops 536870912 | bytes 3670016 | tf_op jit(solution)/shard_map/dot_general | solution.py:34
  9.8 1.9 %collective-permute-done = bf16[4,1,64,512]{3,2,1,0:T(8,128)(2,1)S(1)} collective-permute-done((bf16[4,1,64,512]{3,2,1,0:T(8,128)(2,1)S(1)}, bf16[4,1,64,512]{3,2,1,0:T(8,128)(2,1)S(1)}, u32[]{:S(2)}, u32[]{:S(2)}) %collective-permute-start) | collective-permute-done | bytes 262176 | tf_op jit(solution)/shard_map/ppermute | solution.py:14
  11.7 4.3 %collective-permute-done.1 = bf16[4,1,64,512]{3,2,1,0:T(8,128)(2,1)S(1)} collective-permute-done((bf16[4,1,64,512]{3,2,1,0:T(8,128)(2,1)S(1)}, bf16[4,1,64,512]{3,2,1,0:T(8,128)(2,1)S(1)}, u32[]{:S(2)}, u32[]{:S(2)}) %collective-permute-start.1) | collective-permute-done | bytes 262176 | tf_op jit(solution)/shard_map/ppermute | solution.py:17
  16.0 0.0 copy-done.2
  16.0 0.9 fusion.22
  16.9 0.0 copy-done.4
  16.9 0.7 fusion.35
  17.6 0.7 fusion.37
  18.3 0.7 fusion.39
  19.0 0.7 fusion.41
  19.8 0.7 fusion.43
  20.5 0.7 fusion.23
  21.2 0.7 fusion.27
  21.9 0.0 copy-start.5
  21.9 1.4 %multiply_convert_fusion = bf16[4,4,64,512]{3,2,1,0:T(8,128)(2,1)S(1)} fusion(f32[4,4,64,512]{3,2,1,0:T(8,128)S(1)} %fusion.27, f32[4,4,64,512]{3,2,1,0:T(8,128)S(1)} %fusion.35, f32[4,4,64,512]{3,2,1,0:T(8,128)S(1)} %fusion.37, f32[4,4,64,512]{3,2,1,0:T(8,128)S(1)} %fusion.55, f32[4,4,64,512]{3,2,1,0:T(8,128)S(1)} %fusion.39, ...), kind=kOutput, calls=%fused_computation.25 | convolution fusion | flops 543686656 | bytes 19398656 | tf_op jit(solution)/shard_map/dot_general | solution.py:34
  23.4 1.3 %collective-permute-start.2 = (bf16[2,4,64,512]{3,2,1,0:T(8,128)(2,1)S(1)}, bf16[2,4,64,512]{3,2,1,0:T(8,128)(2,1)S(1)}, u32[]{:S(2)}, u32[]{:S(2)}) collective-permute-start(bf16[2,4,64,512]{3,2,1,0:T(8,128)(2,1)S(1)} %slice.124), channel_id=1, source_target_pairs={{0,4},{4,8},{8,12},{1,5},{5,9},{9,13},{2,6},{6,10},{10,14},{3,7},{... | collective-permute-start | bytes 1572872 | tf_op jit(solution)/shard_map/ppermute | solution.py:25
  24.7 0.0 copy-done.5
  24.7 0.7 fusion.49
  25.4 0.8 collective-permute-done.2
  26.2 0.7 fusion.45
  26.9 0.0 copy-start.6
  26.9 1.0 fusion.5
  27.9 0.0 copy-done.6
  28.0 0.3 fusion.7
  28.3 0.8 copy.22
  29.1 24.7 %all_to_all.30 = bf16[4,4,64,512]{3,1,0,2:T(4,128)(2,1)S(1)} all-to-all(bf16[4,4,64,512]{3,1,0,2:T(4,128)(2,1)S(1)} %copy.22), channel_id=1, replica_groups=mesh['ga'=2,'ta'=4,'gy'=4] {'ta'}, dimensions={2} | all-to-all | bytes 2097152 | tf_op jit(solution)/shard_map/all_to_all | solution.py:107
  53.8 0.6 copy.23
  54.4 0.1 copy.24
  54.4 0.0 copy-done
  54.5 1.8 %convolution_convert_fusion = bf16[1024,1536]{1,0:T(8,128)(2,1)S(1)} fusion(bf16[1024,512]{1,0:T(8,128)(2,1)S(1)} %bitcast.119, bf16[512,1536]{1,0:T(8,128)(2,1)S(1)} %copy-done), kind=kOutput, calls=%fused_computation.5 | convolution fusion | flops 1612185600 | bytes 5767168 | tf_op jit(solution)/shard_map/dot_general | solution.py:63
  56.3 1.7 %fusion.78 = (bf16[16,4,16,512]{3,2,1,0:T(8,128)(2,1)S(1)}, bf16[16,4,16,512]{3,2,1,0:T(8,128)(2,1)}, bf16[16,4,16,512]{3,2,1,0:T(8,128)(2,1)}) fusion(bf16[16,4,16,1536]{3,2,1,0:T(8,128)(2,1)S(1)} %bitcast.117), kind=kLoop, calls=%fused_computation.86 | loop fusion | bytes 6291456 | tf_op jit(solution)/shard_map/slice | solution.py:70
  57.9 2.1 %reshape.84 = bf16[16,4,16,8,64]{4,3,2,1,0:T(8,128)(2,1)} reshape(bf16[16,4,16,512]{3,2,1,0:T(8,128)(2,1)S(1)} %get-tuple-element.5) | data formatting | bytes 2097152 | tf_op jit(solution)/shard_map/reshape | solution.py:89
  60.0 2.8 %reshape.86 = bf16[16,4,16,8,64]{4,3,2,1,0:T(8,128)(2,1)S(1)} reshape(bf16[16,4,16,512]{3,2,1,0:T(8,128)(2,1)} %get-tuple-element.6) | data formatting | bytes 2097152 | tf_op jit(solution)/shard_map/reshape | solution.py:81
  62.8 3.9 %reshape.85 = bf16[16,4,16,8,64]{4,3,2,1,0:T(8,128)(2,1)} reshape(bf16[16,4,16,512]{3,2,1,0:T(8,128)(2,1)} %get-tuple-element.7) | data formatting | bytes 2097152 | tf_op jit(solution)/shard_map/reshape | solution.py:80
  66.7 4.1 %fusion.11 = f32[4,16,8,16,16]{3,4,2,1,0:T(8,128)S(1)} fusion(bf16[16,4,16,8,64]{4,3,2,1,0:T(8,128)(2,1)S(1)} %reshape.86, bf16[16,4,16,8,64]{4,3,2,1,0:T(8,128)(2,1)} %reshape.85), kind=kOutput, calls=%fused_computation.18 | convolution fusion | flops 16777216 | bytes 2621440 | tf_op jit(solution)/shard_map/frwhd,grwhd->rwhfg/dot_general | solution.py:78
  70.8 0.0 copy-start.3
  70.8 17.7 %fusion.80 = (f32[4,16,8,16]{3,2,1,0:T(8,128)S(1)}, f32[4,16,8,16,16]{3,4,2,1,0:T(8,128)S(1)}) fusion(f32[4,16,8,16,16]{3,4,2,1,0:T(8,128)S(1)} %fusion.11), kind=kOutput, calls=%fused_computation.88 | output fusion | flops 524303 | bytes 1081344 | tf_op jit(solution)/shard_map/sub | solution.py:86
  88.6 0.0 copy-done.3
  88.6 1.7 %convert_bitcast_fusion = bf16[16,4,16,8,64]{4,0,3,2,1:T(8,128)(2,1)S(1)} fusion(f32[4,16,8,16,16]{3,4,2,1,0:T(8,128)S(1)} %get-tuple-element.13, f32[4,16,8,16]{3,2,1,0:T(8,128)S(1)} %get-tuple-element.12, bf16[16,4,16,8,64]{4,3,2,1,0:T(8,128)(2,1)S(1)} %copy-done.3), kind=kOutput, calls=%fused_computation.21 | convolution fusion | flops 17563648 | bytes 2654208 | tf_op jit(solution)/shard_map/rwhfg,grwhd->frwhd/dot_general | solution.py:88
  90.3 0.5 copy.29
  90.9 2.0 %convert_element_type.45 = bf16[16,4,16,512]{3,2,1,0:T(8,128)(2,1)} reshape(bf16[16,4,16,8,64]{4,3,2,1,0:T(8,128)(2,1)S(1)} %copy.29) | data formatting | bytes 2097152 | tf_op jit(solution)/shard_map/convert_element_type | solution.py:91
  92.9 0.0 copy-start.7
  92.9 18.0 %all_to_all.31 = bf16[16,4,16,512]{3,2,1,0:T(8,128)(2,1)S(1)} all-to-all(bf16[16,4,16,512]{3,2,1,0:T(8,128)(2,1)} %convert_element_type.45), channel_id=1, replica_groups=mesh['ga'=2,'ta'=4,'gy'=4] {'ta'}, dimensions={0} | all-to-all | bytes 2097152 | tf_op jit(solution)/shard_map/all_to_all | solution.py:96
  111.0 0.1 copy.30
  111.1 0.0 copy-start.1
  111.1 0.0 copy-done.7
  111.1 1.7 %fusion.8 = bf16[4,4,64,512]{3,2,1,0:T(8,128)(2,1)} fusion(bf16[4,4,64,512]{3,2,1,0:T(8,128)(2,1)S(1)} %get-tuple-element.11, bf16[4,4,64,512]{3,2,1,0:T(8,128)(2,1)S(1)} %bitcast.118, bf16[512,512]{1,0:T(8,128)(2,1)S(1)} %copy-done.7), kind=kOutput, calls=%fused_computation.15 | convolution fusion | flops 538443776 | bytes 3670016 | tf_op jit(solution)/shard_map/dot_general | solution.py:110
  112.7 0.0 copy-done.1
  (2 shorter events, 0.0 us)
Async XLA Ops:
  0.0 54.4 %copy-start = (bf16[512,1536]{1,0:T(8,128)(2,1)S(1)}, bf16[512,1536]{1,0:T(8,128)(2,1)}, u32[]{:S(2)}) copy-start(bf16[512,1536]{1,0:T(8,128)(2,1)} %param.9) | copy-start | bytes 4718596
  1.2 10.5 %collective-permute-start = (bf16[4,1,64,512]{3,2,1,0:T(8,128)(2,1)S(1)}, bf16[4,1,64,512]{3,2,1,0:T(8,128)(2,1)S(1)}, u32[]{:S(2)}, u32[]{:S(2)}) collective-permute-start(bf16[4,1,64,512]{3,2,1,0:T(8,128)(2,1)S(1)} %get-tuple-element.8), channel_id=1, source_target_pairs={{0,1},{1,2},{2,3},{4,5},{5,6},{6,7},{8,9},{9,10},{10,11},{12,13},{... | collective-permute-start | bytes 786440 | tf_op jit(solution)/shard_map/ppermute | solution.py:14
  6.2 9.8 %copy-start.2 = (bf16[4,4,64,512]{3,2,1,0:T(8,128)(2,1)S(1)}, bf16[4,4,64,512]{3,2,1,0:T(8,128)(2,1)}, u32[]{:S(2)}) copy-start(bf16[4,4,64,512]{3,2,1,0:T(8,128)(2,1)} %param.6) | copy-start | bytes 3145732
  6.2 9.8 %collective-permute-start.1 = (bf16[4,1,64,512]{3,2,1,0:T(8,128)(2,1)S(1)}, bf16[4,1,64,512]{3,2,1,0:T(8,128)(2,1)S(1)}, u32[]{:S(2)}, u32[]{:S(2)}) collective-permute-start(bf16[4,1,64,512]{3,2,1,0:T(8,128)(2,1)S(1)} %get-tuple-element.9), channel_id=1, source_target_pairs={{1,0},{2,1},{3,2},{5,4},{6,5},{7,6},{9,8},{10,9},{11,10},{13,12},{... | collective-permute-start | bytes 786440 | tf_op jit(solution)/shard_map/ppermute | solution.py:17
  7.6 9.3 %copy-start.4 = (bf16[3,3,512,512]{3,2,1,0:T(8,128)(2,1)S(1)}, bf16[3,3,512,512]{3,2,1,0:T(8,128)(2,1)}, u32[]{:S(2)}) copy-start(bf16[3,3,512,512]{3,2,1,0:T(8,128)(2,1)} %param.7) | copy-start | bytes 14155780
  21.9 2.8 %copy-start.5 = (bf16[3,512,512]{2,1,0:T(8,128)(2,1)S(1)}, bf16[3,512,512]{2,1,0:T(8,128)(2,1)}, u32[]{:S(2)}) copy-start(bf16[3,512,512]{2,1,0:T(8,128)(2,1)} %param.8) | copy-start | bytes 4718596
  23.4 2.8 %collective-permute-start.2 = (bf16[2,4,64,512]{3,2,1,0:T(8,128)(2,1)S(1)}, bf16[2,4,64,512]{3,2,1,0:T(8,128)(2,1)S(1)}, u32[]{:S(2)}, u32[]{:S(2)}) collective-permute-start(bf16[2,4,64,512]{3,2,1,0:T(8,128)(2,1)S(1)} %slice.124), channel_id=1, source_target_pairs={{0,4},{4,8},{8,12},{1,5},{5,9},{9,13},{2,6},{6,10},{10,14},{3,7},{... | collective-permute-start | bytes 1572872 | tf_op jit(solution)/shard_map/ppermute | solution.py:25
  26.9 1.0 copy-start.6
  70.8 17.7 %copy-start.3 = (bf16[16,4,16,8,64]{4,3,2,1,0:T(8,128)(2,1)S(1)}, bf16[16,4,16,8,64]{4,3,2,1,0:T(8,128)(2,1)}, u32[]{:S(2)}) copy-start(bf16[16,4,16,8,64]{4,3,2,1,0:T(8,128)(2,1)} %reshape.84) | copy-start | bytes 3145732
  92.9 18.2 %copy-start.7 = (bf16[512,512]{1,0:T(8,128)(2,1)S(1)}, bf16[512,512]{1,0:T(8,128)(2,1)}, u32[]{:S(2)}) copy-start(bf16[512,512]{1,0:T(8,128)(2,1)} %param.10) | copy-start | bytes 1572868
  111.1 1.7 %copy-start.1 = (bf16[512,1536]{1,0:T(8,128)(2,1)S(1)}, bf16[512,1536]{1,0:T(8,128)(2,1)}, u32[]{:S(2)}) copy-start(bf16[512,1536]{1,0:T(8,128)(2,1)} %param.9) | copy-start | bytes 4718596
where the time goes:
time: 113 us
  blocking collectives  42.7 us (38%)
  matrix products  20.3 us (18%)
  other arithmetic  19 us (17%)
  local copies, waits for them, and re-layouts  15.9 us (14%)
  starting transfers between devices  7.72 us (7%)
  waiting for transfers between devices  6.9 us (6%)
    all_to_all x1, blocking collectives, per_device(): lax.all_to_all(normed, 'ta', split_axis=2, concat_axis=0, tiled=True)  24.7 us
    all_to_all x1, blocking collectives, attend_back(): return lax.all_to_all(output, 'ta', split_axis=0, concat_axis=2, tiled=True)  18 us
    sub x1, other arithmetic, attend(): expo = jnp.exp(scores - peak)  17.7 us
    dot_general x9, matrix products, conv_space(): jnp.dot(window.reshape(-1, channels), w_space[row_off, col_off], preferre...  8.59 us
    ppermute x1, starting transfers between devices, padded_2(): lax.ppermute(lax.slice_in_dim(block, block.shape[dim] - width, None, axis...  4.97 us
    ppermute x1, waiting for transfers between devices, padded_2(): lax.ppermute(lax.slice_in_dim(block, 0, width, axis=dim), axis, backward)  4.27 us
    dot_general x1, matrix products, attend(): jnp.einsum('frwhd,grwhd->rwhfg', queries.reshape(shape), keyset.reshape(s...  4.11 us
    reshape x1, local copies, waits for them, and re-layouts, attend(): queries.reshape(shape)  3.9 us
  transfers between devices with their start and end apart: 3, of which 3 were waited for; matrix products, arithmetic and copies ran while one was open for 3% of the time, Pallas kernels for 0%

commit v1 on v0

--- a/solution.py
+++ b/solution.py
@@ -4,6 +4,22 @@
 from jax.sharding import PartitionSpec as P
 
 HEADS = 8
+
+
+def settle_the_records(unit, axis_key):
+    then, raw_out = (lax.axis_size(axis_key), lax.axis_index(axis_key))
+    seen_now = list(unit.shape)
+    aux = unit.shape[2] // then
+    seen_now[2] = aux
+    r2 = seen_now[0]
+    seen_now[0] = r2 * then
+    x_new = jnp.zeros(seen_now, unit.dtype)
+    for jj in range(then):
+        heard = lax.dynamic_slice_in_dim(unit, (raw_out ^ jj) * aux, aux, axis=2)
+        if jj:
+            heard = lax.ppermute(heard, axis_key, list(map(lambda p: (p, p ^ jj), range(then))))
+        x_new = lax.dynamic_update_slice_in_dim(x_new, heard, (raw_out ^ jj) * r2, axis=0)
+    return x_new
 
 
 def padded_2(block, sides, width):
@@ -103,9 +119,7 @@
     hidden = jax.nn.silu(conv_space(padded, w_space, height, width)).astype(jnp.bfloat16)
     earlier = from_behind(hidden[-2:], "ta", 1)
     mixed, normed = temporal_mix(clip, hidden, earlier, w_time, norm_gain)
-    queries, keyset, valueset = project(
-        lax.all_to_all(normed, "ta", split_axis=2, concat_axis=0, tiled=True), w_qkv
-    )
+    queries, keyset, valueset = project(settle_the_records(normed, "ta"), w_qkv)
     attended = attend_back(queries, keyset, valueset)
     projected = jnp.dot(
         attended.reshape(-1, channels), w_out, preferred_element_type=jnp.float32

time: 113 us -> 101 us (0.89)
  blocking collectives: 42.7 us -> 17.1 us
  other arithmetic: 19 us -> 4.66 us
  waiting for transfers between devices: 6.9 us -> 18.6 us
  starting transfers between devices: 7.72 us -> 16.4 us
  matrix products: 20.3 us -> 25.2 us
  local copies, waits for them, and re-layouts: 15.9 us -> 18.7 us
    all_to_all x1 -> x0, blocking collectives: 24.7 us -> none  [per_device(): lax.all_to_all(normed, 'ta', split_axis=2, concat_axis=0, tiled=True)]
    sub x1, other arithmetic: 17.7 us -> 3.42 us  [attend(): expo = jnp.exp(scores - peak)]
    ppermute x0 -> x3, waiting for transfers between devices: none -> 12.4 us  [settle_the_records(): lax.ppermute(heard, axis_key, list(map(lambda p: (p, p ^ jj), range(then))))]
    ppermute x0 -> x3, starting transfers between devices: none -> 8.73 us  [settle_the_records(): lax.ppermute(heard, axis_key, list(map(lambda p: (p, p ^ jj), range(then))))]
    dot_general x1, matrix products: 1.72 us -> 4.44 us  [attend(): jnp.einsum('rwhfg,grwhd->frwhd', probs, valueset.reshape(shape), preferre...]
    convert_element_type x2, local copies, waits for them, and re-layouts: 2.59 us -> 5.06 us  [attend(): return output.reshape(queries.shape).astype(jnp.bfloat16)]
    dot_general x3, matrix products: 2.4 us -> 3.93 us  [temporal_mix(): jnp.dot(window.reshape(-1, channels), w_time[tap_index], preferred_elemen...]
  transfers between devices with their start and end apart: 3 -> 6, of which waited for: 3 -> 4; matrix products, arithmetic and copies ran while one was open for 3% -> 4% of each run, Pallas kernels for 0% -> 0%
where the time goes in v1:
time: 101 us
  matrix products  25.2 us (25%)
  local copies, waits for them, and re-layouts  18.7 us (19%)
  waiting for transfers between devices  18.6 us (18%)
  blocking collectives  17.1 us (17%)
  starting transfers between devices  16.4 us (16%)
  other arithmetic  4.66 us (5%)
    all_to_all x1, blocking collectives, attend_back(): return lax.all_to_all(output, 'ta', split_axis=0, concat_axis=2, tiled=True)  17.1 us
    ppermute x3, waiting for transfers between devices, settle_the_records(): lax.ppermute(heard, axis_key, list(map(lambda p: (p, p ^ jj), range(then))))  12.4 us
    ppermute x3, starting transfers between devices, settle_the_records(): lax.ppermute(heard, axis_key, list(map(lambda p: (p, p ^ jj), range(then))))  8.73 us
    dot_general x9, matrix products, conv_space(): jnp.dot(window.reshape(-1, channels), w_space[row_off, col_off], preferre...  8.59 us
    convert_element_type x2, local copies, waits for them, and re-layouts, attend(): return output.reshape(queries.shape).astype(jnp.bfloat16)  5.06 us
    ppermute x1, starting transfers between devices, padded_2(): lax.ppermute(lax.slice_in_dim(block, block.shape[dim] - width, None, axis...  4.97 us
    dot_general x1, matrix products, attend(): jnp.einsum('frwhd,grwhd->rwhfg', queries.reshape(shape), keyset.reshape(s...  4.75 us
    dot_general x1, matrix products, attend(): jnp.einsum('rwhfg,grwhd->frwhd', probs, valueset.reshape(shape), preferre...  4.44 us
  transfers between devices with their start and end apart: 6, of which 4 were waited for; matrix products, arithmetic and copies ran while one was open for 4% of the time, Pallas kernels for 0%

profile of v1, /device:TPU:0, one launch (start us, length us, event | category | flops | bytes accessed | tf_op | source)
XLA Modules:
  0.0 101.0 jit_solution(13854898638765052977)
XLA Ops:
  0.0 0.0 copy-start
  0.0 1.2 %fusion.79 = (bf16[4,1,64,512]{3,2,1,0:T(8,128)(2,1)S(1)}, bf16[4,1,64,512]{3,2,1,0:T(8,128)(2,1)S(1)}) fusion(bf16[4,4,64,512]{3,2,1,0:T(8,128)(2,1)} %param.6), kind=kLoop, calls=%fused_computation.94 | loop fusion | bytes 1048576 | tf_op jit(solution)/shard_map/slice | solution.py:31
  1.2 5.0 %collective-permute-start = (bf16[4,1,64,512]{3,2,1,0:T(8,128)(2,1)S(1)}, bf16[4,1,64,512]{3,2,1,0:T(8,128)(2,1)S(1)}, u32[]{:S(2)}, u32[]{:S(2)}) collective-permute-start(bf16[4,1,64,512]{3,2,1,0:T(8,128)(2,1)S(1)} %get-tuple-element.12), channel_id=1, source_target_pairs={{0,1},{1,2},{2,3},{4,5},{5,6},{6,7},{8,9},{9,10},{10,11},{12,13},{... | collective-permute-start | bytes 786440 | tf_op jit(solution)/shard_map/ppermute | solution.py:30
  6.2 0.0 copy-start.2
  6.2 1.4 %collective-permute-start.1 = (bf16[4,1,64,512]{3,2,1,0:T(8,128)(2,1)S(1)}, bf16[4,1,64,512]{3,2,1,0:T(8,128)(2,1)S(1)}, u32[]{:S(2)}, u32[]{:S(2)}) collective-permute-start(bf16[4,1,64,512]{3,2,1,0:T(8,128)(2,1)S(1)} %get-tuple-element.13), channel_id=1, source_target_pairs={{1,0},{2,1},{3,2},{5,4},{6,5},{7,6},{9,8},{10,9},{11,10},{13,12},{... | collective-permute-start | bytes 786440 | tf_op jit(solution)/shard_map/ppermute | solution.py:33
  7.6 0.0 copy-start.7
  7.6 2.2 %fusion.55 = f32[4,4,64,512]{3,2,1,0:T(8,128)S(1)} fusion(bf16[4,4,64,512]{3,2,1,0:T(8,128)(2,1)} %param.6, bf16[3,3,512,512]{3,2,1,0:T(8,128)(2,1)} %param.7), kind=kOutput, calls=%fused_computation.62 | convolution fusion | flops 536870912 | bytes 3670016 | tf_op jit(solution)/shard_map/dot_general | solution.py:50
  9.8 1.9 %collective-permute-done = bf16[4,1,64,512]{3,2,1,0:T(8,128)(2,1)S(1)} collective-permute-done((bf16[4,1,64,512]{3,2,1,0:T(8,128)(2,1)S(1)}, bf16[4,1,64,512]{3,2,1,0:T(8,128)(2,1)S(1)}, u32[]{:S(2)}, u32[]{:S(2)}) %collective-permute-start) | collective-permute-done | bytes 262176 | tf_op jit(solution)/shard_map/ppermute | solution.py:30
  11.7 4.3 %collective-permute-done.1 = bf16[4,1,64,512]{3,2,1,0:T(8,128)(2,1)S(1)} collective-permute-done((bf16[4,1,64,512]{3,2,1,0:T(8,128)(2,1)S(1)}, bf16[4,1,64,512]{3,2,1,0:T(8,128)(2,1)S(1)}, u32[]{:S(2)}, u32[]{:S(2)}) %collective-permute-start.1) | collective-permute-done | bytes 262176 | tf_op jit(solution)/shard_map/ppermute | solution.py:33
  16.0 0.0 copy-done.2
  16.0 0.9 fusion.22
  16.9 0.0 copy-done.7
  16.9 0.7 fusion.35
  17.6 0.7 fusion.37
  18.3 0.7 fusion.39
  19.0 0.7 fusion.41
  19.8 0.7 fusion.43
  20.5 0.7 fusion.23
  21.2 0.7 fusion.27
  21.9 1.4 %multiply_convert_fusion = bf16[4,4,64,512]{3,2,1,0:T(8,128)(2,1)S(1)} fusion(f32[4,4,64,512]{3,2,1,0:T(8,128)S(1)} %fusion.27, f32[4,4,64,512]{3,2,1,0:T(8,128)S(1)} %fusion.35, f32[4,4,64,512]{3,2,1,0:T(8,128)S(1)} %fusion.37, f32[4,4,64,512]{3,2,1,0:T(8,128)S(1)} %fusion.55, f32[4,4,64,512]{3,2,1,0:T(8,128)S(1)} %fusion.39, ...), kind=kOutput, calls=%fused_computation.25 | convolution fusion | flops 543686656 | bytes 19398656 | tf_op jit(solution)/shard_map/dot_general | solution.py:50
  23.3 0.0 copy-start.3
  23.4 1.0 copy-done.3
  24.3 0.8 slice.124
  25.2 1.3 %collective-permute-start.2 = (bf16[2,4,64,512]{3,2,1,0:T(8,128)(2,1)}, bf16[2,4,64,512]{3,2,1,0:T(8,128)(2,1)S(1)}, u32[]{:S(2)}, u32[]{:S(2)}) collective-permute-start(bf16[2,4,64,512]{3,2,1,0:T(8,128)(2,1)} %slice.124), channel_id=1, source_target_pairs={{0,4},{4,8},{8,12},{1,5},{5,9},{9,13},{2,6},{6,10},{10,14},{3,7},{... | collective-permute-start | bytes 1572872 | tf_op jit(solution)/shard_map/ppermute | solution.py:41
  26.5 0.0 copy-start.4
  26.5 0.0 copy-start.8
  26.5 2.2 %fusion.49 = f32[4,4,64,512]{3,2,1,0:T(8,128)S(1)} fusion(bf16[4,4,64,512]{3,2,1,0:T(8,128)(2,1)} %copy-done.3, bf16[3,512,512]{2,1,0:T(8,128)(2,1)} %param.8), kind=kOutput, calls=%fused_computation.56 | convolution fusion | flops 536870912 | bytes 3670016 | tf_op jit(solution)/shard_map/dot_general | solution.py:66
  28.7 0.0 collective-permute-done.2
  28.7 0.0 copy-done.4
  28.8 0.0 copy-done.8
  28.8 0.7 fusion.45
  29.5 0.0 copy-start.9
  29.5 1.0 %fusion.5 = (f32[4,4,64]{2,1,0:T(4,128)S(1)}, bf16[4,4,64,512]{3,2,1,0:T(8,128)(2,1)S(1)}) fusion(bf16[3,512,512]{2,1,0:T(8,128)(2,1)S(1)} %copy-done.8, bf16[4,4,64,512]{3,2,1,0:T(8,128)(2,1)S(1)} %copy-done.4, bf16[2,4,64,512]{3,2,1,0:T(8,128)(2,1)S(1)} %collective-permute-done.2, f32[4,4,64,512]{3,2,1,0:T(8,128)S(1)} %fusion.49, ...), kind=kOutput, calls=%fused_computation.12 | convolution fusion | flops 544209920 | bytes 8392704 | tf_op jit(solution)/shard_map/dot_general | solution.py:66
  30.5 0.0 copy-start.5
  30.5 0.0 copy-done.9
  30.5 0.3 fusion.7
  30.9 0.1 broadcast_in_dim.2
  31.0 0.9 constant_dynamic-slice_fusion
  31.9 0.0 copy-done.5
  31.9 6.4 %collective-permute-start.3 = (bf16[4,4,16,512]{3,2,1,0:T(8,128)(2,1)}, bf16[4,4,16,512]{3,2,1,0:T(8,128)(2,1)S(1)}, u32[]{:S(2)}, u32[]{:S(2)}) collective-permute-start(bf16[4,4,16,512]{3,2,1,0:T(8,128)(2,1)} %get-tuple-element.10), channel_id=1, source_target_pairs={{0,4},{4,0},{8,12},{12,8},{1,5},{5,1},{9,13},{13,9},{2,6},{6,2},{1... | collective-permute-start | bytes 786440 | tf_op jit(solution)/shard_map/ppermute | solution.py:20
  38.3 2.3 %collective-permute-start.4 = (bf16[4,4,16,512]{3,2,1,0:T(8,128)(2,1)}, bf16[4,4,16,512]{3,2,1,0:T(8,128)(2,1)S(1)}, u32[]{:S(2)}, u32[]{:S(2)}) collective-permute-start(bf16[4,4,16,512]{3,2,1,0:T(8,128)(2,1)} %get-tuple-element.9), channel_id=1, source_target_pairs={{0,8},{4,12},{8,0},{12,4},{1,9},{5,13},{9,1},{13,5},{2,10},{6,14},... | collective-permute-start | bytes 786440 | tf_op jit(solution)/shard_map/ppermute | solution.py:20
  40.5 0.1 collective-permute-start.5
  40.6 0.0 collective-permute-done.3
  40.7 7.2 %collective-permute-done.4 = bf16[4,4,16,512]{3,2,1,0:T(8,128)(2,1)S(1)} collective-permute-done((bf16[4,4,16,512]{3,2,1,0:T(8,128)(2,1)}, bf16[4,4,16,512]{3,2,1,0:T(8,128)(2,1)S(1)}, u32[]{:S(2)}, u32[]{:S(2)}) %collective-permute-start.4) | collective-permute-done | bytes 262176 | tf_op jit(solution)/shard_map/ppermute | solution.py:20
  47.9 5.2 %collective-permute-done.5 = bf16[4,4,16,512]{3,2,1,0:T(8,128)(2,1)S(1)} collective-permute-done((bf16[4,4,16,512]{3,2,1,0:T(8,128)(2,1)}, bf16[4,4,16,512]{3,2,1,0:T(8,128)(2,1)S(1)}, u32[]{:S(2)}, u32[]{:S(2)}) %collective-permute-start.5) | collective-permute-done | bytes 262176 | tf_op jit(solution)/shard_map/ppermute | solution.py:20
  53.2 0.0 copy-done
  53.2 1.8 %convolution_convert_fusion = bf16[1024,1536]{1,0:T(8,128)(2,1)S(1)} fusion(bf16[1024,512]{1,0:T(8,128)(2,1)S(1)} %bitcast.114, bf16[512,1536]{1,0:T(8,128)(2,1)S(1)} %copy-done), kind=kOutput, calls=%fused_computation.5 | convolution fusion | flops 1612185600 | bytes 5767168 | tf_op jit(solution)/shard_map/dot_general | solution.py:79
  55.0 1.3 %fusion.78 = (bf16[16,4,16,512]{3,2,1,0:T(8,128)(2,1)S(1)}, bf16[16,4,16,512]{3,2,1,0:T(8,128)(2,1)S(1)}, bf16[16,4,16,512]{3,2,1,0:T(8,128)(2,1)}) fusion(bf16[16,4,16,1536]{3,2,1,0:T(8,128)(2,1)S(1)} %bitcast.113), kind=kLoop, calls=%fused_computation.93 | loop fusion | bytes 6291456 | tf_op jit(solution)/shard_map/slice | solution.py:86
  56.3 3.9 %reshape.84 = bf16[16,4,16,8,64]{4,3,2,1,0:T(8,128)(2,1)} reshape(bf16[16,4,16,512]{3,2,1,0:T(8,128)(2,1)} %get-tuple-element.7) | data formatting | bytes 2097152 | tf_op jit(solution)/shard_map/reshape | solution.py:96
  60.2 2.1 %reshape.85 = bf16[16,4,16,8,64]{4,3,2,1,0:T(8,128)(2,1)} reshape(bf16[16,4,16,512]{3,2,1,0:T(8,128)(2,1)S(1)} %get-tuple-element.6) | data formatting | bytes 2097152 | tf_op jit(solution)/shard_map/reshape | solution.py:97
  62.3 4.7 %fusion.11 = f32[4,16,8,16,16]{3,4,2,1,0:T(8,128)S(1)} fusion(bf16[16,4,16,8,64]{4,3,2,1,0:T(8,128)(2,1)} %reshape.85, bf16[16,4,16,8,64]{4,3,2,1,0:T(8,128)(2,1)} %reshape.84), kind=kOutput, calls=%fused_computation.18 | convolution fusion | flops 16777216 | bytes 2621440 | tf_op jit(solution)/shard_map/frwhd,grwhd->rwhfg/dot_general | solution.py:94
  67.0 3.4 %fusion.80 = (f32[4,16,8,16]{3,2,1,0:T(8,128)S(1)}, f32[4,16,8,16,16]{3,4,2,1,0:T(8,128)}) fusion(f32[4,16,8,16,16]{3,4,2,1,0:T(8,128)S(1)} %fusion.11), kind=kOutput, calls=%fused_computation.95 | output fusion | flops 524303 | bytes 1081344 | tf_op jit(solution)/shard_map/sub | solution.py:102
  70.4 2.1 %reshape.83 = bf16[16,4,16,8,64]{4,3,2,1,0:T(8,128)(2,1)} reshape(bf16[16,4,16,512]{3,2,1,0:T(8,128)(2,1)S(1)} %get-tuple-element.5) | data formatting | bytes 2097152 | tf_op jit(solution)/shard_map/reshape | solution.py:105
  72.5 4.4 %convert_bitcast_fusion = bf16[16,4,16,8,64]{4,0,3,2,1:T(8,128)(2,1)S(1)} fusion(f32[4,16,8,16,16]{3,4,2,1,0:T(8,128)} %get-tuple-element.17, f32[4,16,8,16]{3,2,1,0:T(8,128)S(1)} %get-tuple-element.16, bf16[16,4,16,8,64]{4,3,2,1,0:T(8,128)(2,1)} %reshape.83), kind=kOutput, calls=%fused_computation.21 | convolution fusion | flops 17563648 | bytes 2654208 | tf_op jit(solution)/shard_map/rwhfg,grwhd->frwhd/dot_general | solution.py:104
  77.0 1.9 %copy.12 = bf16[16,4,16,8,64]{4,3,2,1,0:T(8,128)(2,1)} copy(bf16[16,4,16,8,64]{4,0,3,2,1:T(8,128)(2,1)S(1)} %convert_bitcast_fusion) | data formatting | bytes 2097152 | tf_op jit(solution)/shard_map/convert_element_type | solution.py:107
  78.8 3.2 %convert_element_type.45 = bf16[16,4,16,512]{3,2,1,0:T(8,128)(2,1)S(1)} reshape(bf16[16,4,16,8,64]{4,3,2,1,0:T(8,128)(2,1)} %copy.12) | data formatting | bytes 2097152 | tf_op jit(solution)/shard_map/convert_element_type | solution.py:107
  82.0 0.0 copy-start.6
  82.0 0.0 copy-start.10
  82.0 17.1 %all_to_all.15 = bf16[16,4,16,512]{3,2,1,0:T(8,128)(2,1)S(1)} all-to-all(bf16[16,4,16,512]{3,2,1,0:T(8,128)(2,1)S(1)} %convert_element_type.45), channel_id=1, replica_groups=mesh['ga'=2,'ta'=4,'gy'=4] {'ta'}, dimensions={0} | all-to-all | bytes 2097152 | tf_op jit(solution)/shard_map/all_to_all | solution.py:112
  99.1 0.1 copy.13
  99.2 0.0 copy-start.1
  99.3 0.0 copy-done.6
  99.3 0.0 copy-done.10
  99.3 1.7 %fusion.8 = bf16[4,4,64,512]{3,2,1,0:T(8,128)(2,1)} fusion(bf16[4,4,64,512]{3,2,1,0:T(8,128)(2,1)S(1)} %copy-done.6, bf16[4,4,64,512]{3,2,1,0:T(8,128)(2,1)S(1)} %bitcast.115, bf16[512,512]{1,0:T(8,128)(2,1)S(1)} %copy-done.10), kind=kOutput, calls=%fused_computation.15 | convolution fusion | flops 538443776 | bytes 3670016 | tf_op jit(solution)/shard_map/dot_general | solution.py:124
  (5 shorter events, 0.1 us)
Async XLA Ops:
  0.0 53.2 %copy-start = (bf16[512,1536]{1,0:T(8,128)(2,1)S(1)}, bf16[512,1536]{1,0:T(8,128)(2,1)}, u32[]{:S(2)}) copy-start(bf16[512,1536]{1,0:T(8,128)(2,1)} %param.9) | copy-start | bytes 4718596
  1.2 10.5 %collective-permute-start = (bf16[4,1,64,512]{3,2,1,0:T(8,128)(2,1)S(1)}, bf16[4,1,64,512]{3,2,1,0:T(8,128)(2,1)S(1)}, u32[]{:S(2)}, u32[]{:S(2)}) collective-permute-start(bf16[4,1,64,512]{3,2,1,0:T(8,128)(2,1)S(1)} %get-tuple-element.12), channel_id=1, source_target_pairs={{0,1},{1,2},{2,3},{4,5},{5,6},{6,7},{8,9},{9,10},{10,11},{12,13},{... | collective-permute-start | bytes 786440 | tf_op jit(solution)/shard_map/ppermute | solution.py:30
  6.2 9.8 %copy-start.2 = (bf16[4,4,64,512]{3,2,1,0:T(8,128)(2,1)S(1)}, bf16[4,4,64,512]{3,2,1,0:T(8,128)(2,1)}, u32[]{:S(2)}) copy-start(bf16[4,4,64,512]{3,2,1,0:T(8,128)(2,1)} %param.6) | copy-start | bytes 3145732
  6.2 9.8 %collective-permute-start.1 = (bf16[4,1,64,512]{3,2,1,0:T(8,128)(2,1)S(1)}, bf16[4,1,64,512]{3,2,1,0:T(8,128)(2,1)S(1)}, u32[]{:S(2)}, u32[]{:S(2)}) collective-permute-start(bf16[4,1,64,512]{3,2,1,0:T(8,128)(2,1)S(1)} %get-tuple-element.13), channel_id=1, source_target_pairs={{1,0},{2,1},{3,2},{5,4},{6,5},{7,6},{9,8},{10,9},{11,10},{13,12},{... | collective-permute-start | bytes 786440 | tf_op jit(solution)/shard_map/ppermute | solution.py:33
  7.6 9.3 %copy-start.7 = (bf16[3,3,512,512]{3,2,1,0:T(8,128)(2,1)S(1)}, bf16[3,3,512,512]{3,2,1,0:T(8,128)(2,1)}, u32[]{:S(2)}) copy-start(bf16[3,3,512,512]{3,2,1,0:T(8,128)(2,1)} %param.7) | copy-start | bytes 14155780
  23.3 1.0 copy-start.3
  25.2 3.6 %collective-permute-start.2 = (bf16[2,4,64,512]{3,2,1,0:T(8,128)(2,1)}, bf16[2,4,64,512]{3,2,1,0:T(8,128)(2,1)S(1)}, u32[]{:S(2)}, u32[]{:S(2)}) collective-permute-start(bf16[2,4,64,512]{3,2,1,0:T(8,128)(2,1)} %slice.124), channel_id=1, source_target_pairs={{0,4},{4,8},{8,12},{1,5},{5,9},{9,13},{2,6},{6,10},{10,14},{3,7},{... | collective-permute-start | bytes 1572872 | tf_op jit(solution)/shard_map/ppermute | solution.py:41
  26.5 2.2 %copy-start.4 = (bf16[4,4,64,512]{3,2,1,0:T(8,128)(2,1)S(1)}, bf16[4,4,64,512]{3,2,1,0:T(8,128)(2,1)}, u32[]{:S(2)}) copy-start(bf16[4,4,64,512]{3,2,1,0:T(8,128)(2,1)} %copy-done.3) | copy-start | bytes 3145732
  26.5 2.2 %copy-start.8 = (bf16[3,512,512]{2,1,0:T(8,128)(2,1)S(1)}, bf16[3,512,512]{2,1,0:T(8,128)(2,1)}, u32[]{:S(2)}) copy-start(bf16[3,512,512]{2,1,0:T(8,128)(2,1)} %param.8) | copy-start | bytes 4718596
  29.5 1.1 %copy-start.9 = (f32[512]{0:T(512)S(1)}, f32[512]{0:T(512)}, u32[]{:S(2)}) copy-start(f32[512]{0:T(512)} %param.11) | copy-start | bytes 6148
  30.5 1.4 %copy-start.5 = (bf16[4,4,64,512]{3,2,1,0:T(8,128)(2,1)}, bf16[4,4,64,512]{3,2,1,0:T(8,128)(2,1)S(1)}, u32[]{:S(2)}) copy-start(bf16[4,4,64,512]{3,2,1,0:T(8,128)(2,1)S(1)} %get-tuple-element.15) | copy-start | bytes 3145732
  31.9 8.7 %collective-permute-start.3 = (bf16[4,4,16,512]{3,2,1,0:T(8,128)(2,1)}, bf16[4,4,16,512]{3,2,1,0:T(8,128)(2,1)S(1)}, u32[]{:S(2)}, u32[]{:S(2)}) collective-permute-start(bf16[4,4,16,512]{3,2,1,0:T(8,128)(2,1)} %get-tuple-element.10), channel_id=1, source_target_pairs={{0,4},{4,0},{8,12},{12,8},{1,5},{5,1},{9,13},{13,9},{2,6},{6,2},{1... | collective-permute-start | bytes 786440 | tf_op jit(solution)/shard_map/ppermute | solution.py:20
  38.3 9.6 %collective-permute-start.4 = (bf16[4,4,16,512]{3,2,1,0:T(8,128)(2,1)}, bf16[4,4,16,512]{3,2,1,0:T(8,128)(2,1)S(1)}, u32[]{:S(2)}, u32[]{:S(2)}) collective-permute-start(bf16[4,4,16,512]{3,2,1,0:T(8,128)(2,1)} %get-tuple-element.9), channel_id=1, source_target_pairs={{0,8},{4,12},{8,0},{12,4},{1,9},{5,13},{9,1},{13,5},{2,10},{6,14},... | collective-permute-start | bytes 786440 | tf_op jit(solution)/shard_map/ppermute | solution.py:20
  40.5 12.6 %collective-permute-start.5 = (bf16[4,4,16,512]{3,2,1,0:T(8,128)(2,1)}, bf16[4,4,16,512]{3,2,1,0:T(8,128)(2,1)S(1)}, u32[]{:S(2)}, u32[]{:S(2)}) collective-permute-start(bf16[4,4,16,512]{3,2,1,0:T(8,128)(2,1)} %get-tuple-element.8), channel_id=1, source_target_pairs={{0,12},{4,8},{8,4},{12,0},{1,13},{5,9},{9,5},{13,1},{2,14},{6,10},... | collective-permute-start | bytes 786440 | tf_op jit(solution)/shard_map/ppermute | solution.py:20
  82.0 17.2 %copy-start.6 = (bf16[4,4,64,512]{3,2,1,0:T(8,128)(2,1)S(1)}, bf16[4,4,64,512]{3,2,1,0:T(8,128)(2,1)}, u32[]{:S(2)}) copy-start(bf16[4,4,64,512]{3,2,1,0:T(8,128)(2,1)} %copy-done.5) | copy-start | bytes 3145732
  82.0 17.2 %copy-start.10 = (bf16[512,512]{1,0:T(8,128)(2,1)S(1)}, bf16[512,512]{1,0:T(8,128)(2,1)}, u32[]{:S(2)}) copy-start(bf16[512,512]{1,0:T(8,128)(2,1)} %param.10) | copy-start | bytes 1572868
  99.2 1.7 %copy-start.1 = (bf16[512,1536]{1,0:T(8,128)(2,1)S(1)}, bf16[512,1536]{1,0:T(8,128)(2,1)}, u32[]{:S(2)}) copy-start(bf16[512,1536]{1,0:T(8,128)(2,1)} %param.9) | copy-start | bytes 4718596
